TPU v7x, 512 devices: a whole 4x4x16 slice. The times are simulated.
512 devices in a mesh: aux: 16 (over z_lo, y), row: 32 (over x, z_hi, core).
Axes of the slice: x: 4, y: 4, z: 16 (z_hi: 4, z_lo: 4; z = z_hi * 4 + z_lo), core: 2. Of those that a mesh axis runs over, the one named last changes fastest.
Arguments:
- coeff: bfloat16 [800, 4096], P(None, 'row'), may hold values from -0.109375 to 0.109375
- band: bfloat16 [32, 384, 4096], P('aux', None, 'row'), may hold values from -6 to 6
- pairs: int32 [32, 32], replicated, may hold values from 0 to 1, as said below
Outputs:
- exchange_k: float32 [4096, 4096], P('row', 'aux')
Inputs may be any that keep to these rules, and one draw needn't show every extreme that they name: pairs is symmetric, holds only 0 and 1, and its diagonal is 1; how many blocks a row keeps differs from row to row.
All inputs are finite; a program needn't handle non-finite values.
Results may differ from a plain program's by a relative error of at most 0.0012.
Values may be sent and summed in bfloat16 or wider, within the bound.
No kernel may reach another device: no remote copies, remote signals or barrier semaphores. Data moves between devices by JAX's collectives and lax.ppermute only.
A program may use at most 64 MiB of HBM per device.

v0:
```python
import math

import jax
import jax.numpy as jnp
from jax import lax
from jax.experimental import pallas as pl
from jax.experimental.pallas import tpu as pltpu
from jax.sharding import Mesh
from jax.sharding import PartitionSpec as P


AUX = ("zl", "y")
ROW = ("x", "zh", "c")
ALONG_Z = [(4 * zl + zh, 4 * zl + (zh + (1, 3)[zl % 2]) % 4) for zl in range(4) for zh in range(4)]


def shifted(value, axis, step):
    count = lax.axis_size(axis)
    return lax.ppermute(value, axis, [(i, (i + step) % count) for i in range(count)])


def is_even():
    return lax.rem(lax.axis_index("zl"), 2) == 0


def own_part(coeff, band, sides, made):
    block = coeff.shape[1]
    start = 2 * block * lax.axis_index("c")
    for row, side in enumerate((start, 2 * block - start)):
        for q in range(2):
            sides[row * block : (row + 1) * block, q * block : (q + 1) * block] = band[
                q, pl.ds(side, block)
            ]
    middle = jnp.concatenate([band[q, block : 2 * block] for q in range(2)], axis=1)
    made[...] = jnp.dot(coeff[...], middle, preferred_element_type=jnp.float32)


def half_block(outer, partner, sides, made, half, copies, sems):
    nocc, block = outer.shape
    window = jnp.concatenate([outer[...], partner[...]], axis=1)
    whole = made[...] + jnp.dot(window, sides[...], preferred_element_type=jnp.float32)
    for q in range(2):
        half[q * nocc : (q + 1) * nocc] = whole[:, q * block : (q + 1) * block].astype(half.dtype)
    sent = [pltpu.make_async_copy(half, copies.at[k], sems.at[k]) for k in range(4)]
    for copy in sent:
        copy.start()
    for copy in sent:
        copy.wait()


def kept_out(kernel):
    def run(*refs):
        *inputs, out, made, sem = refs
        kernel(*inputs, made)
        copy = pltpu.make_async_copy(made, out, sem)
        copy.start()
        copy.wait()

    return run


def tiles_of(columns, mine):
    block = mine.shape[2]
    made = lax.dot_general(
        jnp.concatenate([column[...] for column in columns], axis=1),
        jnp.concatenate([mine[k] for k in range(4)], axis=1),
        (((0,), (0,)), ((), ())),
        preferred_element_type=jnp.float32,
    )
    for k in range(4):
        yield (
            k,
            [
                made[j * block : (j + 1) * block, k * block : (k + 1) * block]
                for j in range(len(columns))
            ],
        )


def by_parity(store, tile):
    even = is_even()
    pl.when(even)(lambda: store(tile))
    pl.when(jnp.logical_not(even))(lambda: store(tile.T))


def first_tiles(own_other, near, near_other, mine, slices):
    cut = slices.shape[4]
    core = lax.axis_index("c")
    own = mine.at[lax.axis_index("x")]
    for k, made in tiles_of((own, own_other, near, near_other), mine):
        for side in range(2):

            def put(kind, tile, to=(core + side) % 2, k=k):
                for s in range(4):
                    slices[s, to, kind, k] = tile[s * cut : (s + 1) * cut]

            put(0, made[side])
            by_parity(lambda tile, put=put: put(1, tile), made[2 + side])


def patch_tiles(near, near_other, far, far_other, mine, patch):
    cut = patch.shape[4]
    core = lax.axis_index("c")
    for k, made in tiles_of((near, near_other, far, far_other), mine):
        for side in range(2):

            def put(kind, tile, of=(core + side) % 2, k=k):
                for s in range(4):
                    patch[s, k, kind, of] = tile[s * cut : (s + 1) * cut]

            put(1, made[2 + side])
            by_parity(lambda tile, put=put: put(0, tile), made[side])


def near_summed(early, out):
    for c in range(2):
        for k in range(4):
            out[c, k] = early[0, c, 1, k] + early[1, c, 1, k] + early[2, c, 1, k] + early[3, c, 1, k]


def placed(early, mirrored, arrived, parts):
    zh = lax.axis_index("zh")
    toward = jnp.where(is_even(), 3, 1)
    homes = (lax.rem(zh + toward, 4), lax.rem(zh + 2, 4))
    for j in range(4):
        for c in range(2):
            parts[j, zh, c] = early[0, c, 0, j] + early[1, c, 0, j] + early[2, c, 0, j] + early[3, c, 0, j]
            parts[j, lax.rem(zh + 4 - toward, 4), c] = mirrored[c, j]
            for kind in range(2):
                parts[j, homes[kind], c] = (
                    arrived[0, j, kind, c]
                    + arrived[1, j, kind, c]
                    + arrived[2, j, kind, c]
                    + arrived[3, j, kind, c]
                )


def finished(pairs, total, out):
    block = out.shape[0]
    row = 8 * lax.axis_index("x") + 2 * lax.axis_index("zh") + lax.axis_index("c")
    first = 8 * lax.axis_index("zl") + 2 * lax.axis_index("y")
    straight = lax.rem(lax.axis_index("y") + 4 - lax.axis_index("zh"), 4) < 2
    for c in range(2):
        keep = pairs[row, first + c].astype(jnp.float32)
        tile = (total[0, :, c] + total[1, :, c] + total[2, :, c] + total[3, :, c]) * keep
        tile = tile.reshape(block, block)

        @pl.when(straight)
        def _(tile=tile, c=c):
            out[:, c * block : (c + 1) * block] = tile

        @pl.when(jnp.logical_not(straight))
        def _(tile=tile, c=c):
            out[:, c * block : (c + 1) * block] = tile.T


def local(kernel, results, flops, *arrays, scalars=0, out=False):
    whole = pl.BlockSpec(memory_space=pltpu.VMEM)
    table = pl.BlockSpec(memory_space=pltpu.SMEM)
    shapes = [
        pltpu.HBM(shape, kind) if space == pltpu.HBM else jax.ShapeDtypeStruct(shape, kind)
        for shape, kind, space in results
    ]
    scratch = []
    if out:
        kernel = kept_out(kernel)
        scratch = [pltpu.VMEM(*results[0][:2]), pltpu.SemaphoreType.DMA(())]
    elif any(space == pltpu.HBM for *_, space in results):
        scratch = [pltpu.SemaphoreType.DMA((4,))]
    moved = sum(a.size * a.dtype.itemsize for a in arrays)
    moved += sum(math.prod(shape) * jnp.dtype(kind).itemsize for shape, kind, _ in results)
    return pl.pallas_call(
        kernel,
        out_shape=shapes,
        in_specs=[table] * scalars + [whole] * (len(arrays) - scalars),
        out_specs=[pl.BlockSpec(memory_space=space) for *_, space in results],
        scratch_shapes=scratch,
        cost_estimate=pl.CostEstimate(flops=flops, bytes_accessed=moved, transcendentals=0),
        compiler_params=pltpu.CompilerParams(vmem_limit_bytes=2 * moved + (8 << 20)),
    )(*arrays)


def patch_sums(coeff, band, pairs):
    nocc, block = coeff.shape
    cut = block // 4

    count = lax.axis_size(ROW)
    partner = shifted(coeff, "c", 1)
    outward = [(r, r + 1) for r in range(1, count - 1, 2)]
    outer = lax.ppermute(coeff, ROW, outward + [(b, a) for a, b in outward])
    depth = band.shape[0] * nocc
    wide = band.shape[0] * block
    vmem, hbm = pltpu.VMEM, pltpu.HBM
    sides, made = local(
        own_part,
        [((2 * block, wide), jnp.bfloat16, vmem), ((nocc, wide), jnp.float32, vmem)],
        2 * nocc * block * wide,
        coeff,
        band,
    )
    half, copies = local(
        half_block,
        [((depth, block), jnp.bfloat16, vmem), ((4, depth, block), jnp.bfloat16, hbm)],
        4 * nocc * block * wide,
        outer,
        partner,
        sides,
        made,
    )

    near = lax.ppermute(half, ("zl", "zh"), ALONG_Z)
    mine = lax.all_to_all(copies, "x", split_axis=0, concat_axis=0, tiled=True)
    own_other = shifted(half, "c", 1)
    far = lax.ppermute(near, ("zl", "zh"), ALONG_Z)
    near_other = shifted(near, "c", 1)
    far_other = shifted(far, "c", 1)

    def summed(tiles, axes):
        return lax.all_to_all(tiles, axes, split_axis=0, concat_axis=0, tiled=True)

    work = 2 * half.shape[0] * block * 16 * block
    (slices,) = local(
        first_tiles,
        [((4, 2, 2, 4, cut, block), jnp.float32, hbm)],
        work,
        own_other,
        near,
        near_other,
        mine,
        out=True,
    )
    early = summed(slices.reshape(8, 8 * cut, block), ("y", "c"))
    early = early.reshape(4, 2, 2, 4, cut, block)
    (mirrored,) = local(near_summed, [((2, 4, cut, block), jnp.float32, vmem)], 0, early)
    mirrored = lax.ppermute(mirrored, ("zl", "zh"), [(b, a) for a, b in ALONG_Z])
    (patch,) = local(
        patch_tiles,
        [((4, 4, 2, 2, cut, block), jnp.float32, hbm)],
        work,
        near,
        near_other,
        far,
        far_other,
        mine,
        out=True,
    )
    arrived = summed(patch.reshape(16, 4 * cut, block), ("y", "x"))
    arrived = arrived.reshape(4, 4, 2, 2, cut, block)
    (parts,) = local(
        placed, [((4, 4, 2, cut, block), jnp.float32, vmem)], 0, early, mirrored, arrived
    )
    total = lax.all_to_all(
        parts.reshape(16, 2 * cut, block), AUX, split_axis=0, concat_axis=0, tiled=True
    )
    total = total.reshape(4, 4, 2, cut, block)
    (out,) = local(
        finished, [((block, 2 * block), jnp.float32, vmem)], 0, pairs, total, scalars=1
    )
    return out


def solution(mesh):
    torus = Mesh(mesh.devices.reshape(4, 4, 4, 4, 2), ("zl", "y", "x", "zh", "c"))
    in_specs = (P(None, ROW), P(AUX, None, ROW), P())
    return jax.shard_map(
        patch_sums, mesh=torus, in_specs=in_specs, out_specs=P(ROW, AUX), check_vma=False
    )
```

profile of v0, /device:TPU:6, one launch (start us, length us, event | category | flops | bytes accessed | tf_op | source)
XLA Modules:
  0.0 135.4 jit_solution(9954897150341381493)
XLA Ops:
  0.0 12.4 %collective-permute-start = (bf16[800,128]{1,0:T(8,128)(2,1)}, bf16[800,128]{1,0:T(8,128)(2,1)S(1)}, u32[]{:S(2)}, u32[]{:S(2)}) collective-permute-start(bf16[800,128]{1,0:T(8,128)(2,1)} %coeff.1), channel_id=1, source_target_pairs={{1,2},{3,4},{5,6},{7,8},{9,10},{11,12},{13,14},{15,16},{17,18},{19... | collective-permute-start | bytes 614408 | tf_op jit(solution)/shard_map/ppermute | solution.py:190
  12.4 1.9 %collective-permute-start.1 = (bf16[800,128]{1,0:T(8,128)(2,1)}, bf16[800,128]{1,0:T(8,128)(2,1)S(1)}, u32[]{:S(2)}, u32[]{:S(2)}) collective-permute-start(bf16[800,128]{1,0:T(8,128)(2,1)} %coeff.1), channel_id=1, source_target_pairs={{0,1},{1,0},{2,3},{3,2},{4,5},{5,4},{6,7},{7,6},{8,9},{9,8},{10,11... | collective-permute-start | bytes 614408 | tf_op jit(solution)/shard_map/ppermute | solution.py:19
  14.4 0.0 copy-start
  14.4 0.9 copy-done
  15.3 0.9 copy-done.1
  16.2 0.3 shard_map.37
  16.5 6.1 %collective-permute-done.outer = bf16[800,128]{1,0:T(8,128)(2,1)S(1)} collective-permute-done((bf16[800,128]{1,0:T(8,128)(2,1)}, bf16[800,128]{1,0:T(8,128)(2,1)S(1)}, u32[]{:S(2)}, u32[]{:S(2)}) %collective-permute-start) | collective-permute-done | bytes 204832 | tf_op jit(solution)/shard_map/ppermute | solution.py:190
  22.6 0.0 collective-permute-done.1.partner
  22.6 1.5 %shard_map.38 = (bf16[1600,128]{1,0:T(8,128)(2,1)S(1)}, bf16[4,1600,128]{2,1,0:T(8,128)(2,1)}) custom-call(bf16[800,128]{1,0:T(8,128)(2,1)S(1)} %collective-permute-done.outer, bf16[800,128]{1,0:T(8,128)(2,1)S(1)} %collective-permute-done.1.partner, bf16[256,256]{1,0:T(8,128)(2,1)S(1)} %get-tuple-element.9.sides, f32[800,256]{1,0:T(8,128)S(1)} %get-tuple-element.10.made), custom_call_target="tpu_custom_call" | custom-call | flops 104857600 | bytes 3407872 | tf_op jit(solution)/shard_map/pallas_call | solution.py:172
  24.1 4.5 %all-to-all-start = ((bf16[4,1600,128]{2,1,0:T(8,128)(2,1)}), bf16[4,1600,128]{2,1,0:T(8,128)(2,1)S(1)}, u32[]{:S(2)}, u32[]{:S(2)}) async-start(bf16[4,1600,128]{2,1,0:T(8,128)(2,1)} %get-tuple-element.12), calls=%async_computation | async-start | bytes 3276800 | tf_op jit(solution)/shard_map/all_to_all | solution.py:212
  28.6 1.9 %collective-permute-start.3 = (bf16[1600,128]{1,0:T(8,128)(2,1)S(1)}, bf16[1600,128]{1,0:T(8,128)(2,1)S(1)}, u32[]{:S(2)}, u32[]{:S(2)}) collective-permute-start(bf16[1600,128]{1,0:T(8,128)(2,1)S(1)} %get-tuple-element.11), channel_id=1, source_target_pairs={{0,2},{2,4},{4,6},{6,0},{128,134},{130,128},{132,130},{134,132},{2... | collective-permute-start | bytes 1228808 | tf_op jit(solution)/shard_map/ppermute | solution.py:211
  30.6 5.3 %collective-permute-start.2 = (bf16[1600,128]{1,0:T(8,128)(2,1)S(1)}, bf16[1600,128]{1,0:T(8,128)(2,1)S(1)}, u32[]{:S(2)}, u32[]{:S(2)}) collective-permute-start(bf16[1600,128]{1,0:T(8,128)(2,1)S(1)} %get-tuple-element.11), channel_id=1, source_target_pairs={{0,1},{1,0},{2,3},{3,2},{4,5},{5,4},{6,7},{7,6},{8,9},{9,8},{10,11... | collective-permute-start | bytes 1228808 | tf_op jit(solution)/shard_map/ppermute | solution.py:19
  35.9 19.6 %collective-permute-done.3.refs_1_.refs_0_ = bf16[1600,128]{1,0:T(8,128)(2,1)S(1)} collective-permute-done((bf16[1600,128]{1,0:T(8,128)(2,1)S(1)}, bf16[1600,128]{1,0:T(8,128)(2,1)S(1)}, u32[]{:S(2)}, u32[]{:S(2)}) %collective-permute-start.3) | collective-permute-done | bytes 409632 | tf_op jit(solution)/shard_map/ppermute | solution.py:211
  55.4 1.9 %collective-permute-start.4 = (bf16[1600,128]{1,0:T(8,128)(2,1)S(1)}, bf16[1600,128]{1,0:T(8,128)(2,1)S(1)}, u32[]{:S(2)}, u32[]{:S(2)}) collective-permute-start(bf16[1600,128]{1,0:T(8,128)(2,1)S(1)} %collective-permute-done.3.refs_1_.refs_0_), channel_id=1, source_target_pairs={{0,1},{1,0},{2,3},{3,2},{4,5},{5,4},{6,7},{7,6},{8,9},{9,8},{10,11... | collective-permute-start | bytes 1228808 | tf_op jit(solution)/shard_map/ppermute | solution.py:19
  57.4 0.0 collective-permute-done.2.refs_0_
  57.4 1.7 %collective-permute-done.4.refs_2_.refs_1_ = bf16[1600,128]{1,0:T(8,128)(2,1)S(1)} collective-permute-done((bf16[1600,128]{1,0:T(8,128)(2,1)S(1)}, bf16[1600,128]{1,0:T(8,128)(2,1)S(1)}, u32[]{:S(2)}, u32[]{:S(2)}) %collective-permute-start.4) | collective-permute-done | bytes 409632 | tf_op jit(solution)/shard_map/ppermute | solution.py:19
  59.1 0.0 all-to-all-done.refs_3_.refs_4_
  59.1 2.2 %shard_map.39 = f32[4,2,2,4,32,128]{5,4,3,2,1,0:T(8,128)} custom-call(bf16[1600,128]{1,0:T(8,128)(2,1)S(1)} %collective-permute-done.2.refs_0_, bf16[1600,128]{1,0:T(8,128)(2,1)S(1)} %collective-permute-done.3.refs_1_.refs_0_, bf16[1600,128]{1,0:T(8,128)(2,1)S(1)} %collective-permute-done.4.refs_2_.refs_1_, ...), custom_call_target="tpu_custom_call" | custom-call | flops 838860800 | bytes 3915776 | tf_op jit(solution)/shard_map/pallas_call | solution.py:172
  61.3 4.5 %all-to-all-start.1 = ((f32[8,256,128]{2,1,0:T(8,128)}), f32[8,256,128]{2,1,0:T(8,128)S(1)}, u32[]{:S(2)}, u32[]{:S(2)}) async-start(f32[8,256,128]{2,1,0:T(8,128)} %bitcast.11), calls=%async_computation.1 | async-start | bytes 2097152 | tf_op jit(solution)/shard_map/all_to_all | solution.py:219
  65.8 1.9 %collective-permute-start.6 = (bf16[1600,128]{1,0:T(8,128)(2,1)S(1)}, bf16[1600,128]{1,0:T(8,128)(2,1)S(1)}, u32[]{:S(2)}, u32[]{:S(2)}) collective-permute-start(bf16[1600,128]{1,0:T(8,128)(2,1)S(1)} %collective-permute-done.3.refs_1_.refs_0_), channel_id=1, source_target_pairs={{0,2},{2,4},{4,6},{6,0},{128,134},{130,128},{132,130},{134,132},{2... | collective-permute-start | bytes 1228808 | tf_op jit(solution)/shard_map/ppermute | solution.py:214
  67.7 20.4 %collective-permute-done.6.refs_2_ = bf16[1600,128]{1,0:T(8,128)(2,1)S(1)} collective-permute-done((bf16[1600,128]{1,0:T(8,128)(2,1)S(1)}, bf16[1600,128]{1,0:T(8,128)(2,1)S(1)}, u32[]{:S(2)}, u32[]{:S(2)}) %collective-permute-start.6) | collective-permute-done | bytes 409632 | tf_op jit(solution)/shard_map/ppermute | solution.py:214
  88.1 2.0 %collective-permute-start.7 = (bf16[1600,128]{1,0:T(8,128)(2,1)S(1)}, bf16[1600,128]{1,0:T(8,128)(2,1)S(1)}, u32[]{:S(2)}, u32[]{:S(2)}) collective-permute-start(bf16[1600,128]{1,0:T(8,128)(2,1)S(1)} %collective-permute-done.6.refs_2_), channel_id=1, source_target_pairs={{0,1},{1,0},{2,3},{3,2},{4,5},{5,4},{6,7},{7,6},{8,9},{9,8},{10,11... | collective-permute-start | bytes 1228808 | tf_op jit(solution)/shard_map/ppermute | solution.py:19
  90.1 1.7 %collective-permute-done.7.refs_3_ = bf16[1600,128]{1,0:T(8,128)(2,1)S(1)} collective-permute-done((bf16[1600,128]{1,0:T(8,128)(2,1)S(1)}, bf16[1600,128]{1,0:T(8,128)(2,1)S(1)}, u32[]{:S(2)}, u32[]{:S(2)}) %collective-permute-start.7) | collective-permute-done | bytes 409632 | tf_op jit(solution)/shard_map/ppermute | solution.py:19
  91.7 2.2 %shard_map.41 = f32[4,4,2,2,32,128]{5,4,3,2,1,0:T(8,128)} custom-call(bf16[1600,128]{1,0:T(8,128)(2,1)S(1)} %collective-permute-done.3.refs_1_.refs_0_, bf16[1600,128]{1,0:T(8,128)(2,1)S(1)} %collective-permute-done.4.refs_2_.refs_1_, bf16[1600,128]{1,0:T(8,128)(2,1)S(1)} %collective-permute-done.6.refs_2_, ...), custom_call_target="tpu_custom_call" | custom-call | flops 838860800 | bytes 4325376 | tf_op jit(solution)/shard_map/pallas_call | solution.py:172
  94.0 0.0 all-to-all-done.1
  94.0 7.4 %all-to-all-start.2 = ((f32[16,128,128]{2,1,0:T(8,128)}), f32[16,128,128]{2,1,0:T(8,128)S(1)}, u32[]{:S(2)}, u32[]{:S(2)}) async-start(f32[16,128,128]{2,1,0:T(8,128)} %bitcast.12), calls=%async_computation.2 | async-start | bytes 2097152 | tf_op jit(solution)/shard_map/all_to_all | solution.py:219
  101.4 5.5 %collective-permute-start.5 = (f32[2,4,32,128]{3,2,1,0:T(8,128)S(1)}, f32[2,4,32,128]{3,2,1,0:T(8,128)S(1)}, u32[]{:S(2)}, u32[]{:S(2)}) collective-permute-start(f32[2,4,32,128]{3,2,1,0:T(8,128)S(1)} %shard_map.40), channel_id=1, source_target_pairs={{2,0},{4,2},{6,4},{0,6},{134,128},{128,130},{130,132},{132,134},{2... | collective-permute-start | bytes 393224 | tf_op jit(solution)/shard_map/ppermute | solution.py:235
  106.9 9.3 %all-to-all-done.2 = f32[16,128,128]{2,1,0:T(8,128)S(1)} async-done(((f32[16,128,128]{2,1,0:T(8,128)}), f32[16,128,128]{2,1,0:T(8,128)S(1)}, u32[]{:S(2)}, u32[]{:S(2)}) %all-to-all-start.2) | async-done | bytes 1048608 | tf_op jit(solution)/shard_map/all_to_all | solution.py:219
  116.2 0.0 collective-permute-done.5.mirrored
  116.2 0.1 shard_map.42
  116.3 17.6 %all_to_all.20 = f32[16,64,128]{2,1,0:T(8,128)S(1)} all-to-all(f32[16,64,128]{2,1,0:T(8,128)S(1)} %bitcast.10), channel_id=1, replica_groups=mesh['zl'=4,'y'=4,'x'=4,'zh'=4,'c'=2] {'zl','y'}, dimensions={0} | all-to-all | bytes 1048576 | tf_op jit(solution)/shard_map/all_to_all | solution.py:252
  133.9 1.5 %shard_map.43 = f32[128,256]{1,0:T(8,128)} custom-call(s32[32,32]{1,0:T(8,128)S(1)} %copy-done.2, f32[4,4,2,32,128]{4,3,2,1,0:T(8,128)S(1)} %bitcast.9), custom_call_target="tpu_custom_call" | custom-call | bytes 659456 | tf_op jit(solution)/shard_map/pallas_call | solution.py:172
  (4 shorter events, 0.0 us)
Async XLA Ops:
  0.0 22.6 %collective-permute-start = (bf16[800,128]{1,0:T(8,128)(2,1)}, bf16[800,128]{1,0:T(8,128)(2,1)S(1)}, u32[]{:S(2)}, u32[]{:S(2)}) collective-permute-start(bf16[800,128]{1,0:T(8,128)(2,1)} %coeff.1), channel_id=1, source_target_pairs={{1,2},{3,4},{5,6},{7,8},{9,10},{11,12},{13,14},{15,16},{17,18},{19... | collective-permute-start | bytes 614408 | tf_op jit(solution)/shard_map/ppermute | solution.py:190
  12.4 10.2 %collective-permute-start.1 = (bf16[800,128]{1,0:T(8,128)(2,1)}, bf16[800,128]{1,0:T(8,128)(2,1)S(1)}, u32[]{:S(2)}, u32[]{:S(2)}) collective-permute-start(bf16[800,128]{1,0:T(8,128)(2,1)} %coeff.1), channel_id=1, source_target_pairs={{0,1},{1,0},{2,3},{3,2},{4,5},{5,4},{6,7},{7,6},{8,9},{9,8},{10,11... | collective-permute-start | bytes 614408 | tf_op jit(solution)/shard_map/ppermute | solution.py:19
  14.4 0.9 copy-start
  15.3 0.9 copy-start.1
  24.1 34.9 %all-to-all-start = ((bf16[4,1600,128]{2,1,0:T(8,128)(2,1)}), bf16[4,1600,128]{2,1,0:T(8,128)(2,1)S(1)}, u32[]{:S(2)}, u32[]{:S(2)}) async-start(bf16[4,1600,128]{2,1,0:T(8,128)(2,1)} %get-tuple-element.12), calls=%async_computation | async-start | bytes 3276800 | tf_op jit(solution)/shard_map/all_to_all | solution.py:212
  28.6 26.8 %collective-permute-start.3 = (bf16[1600,128]{1,0:T(8,128)(2,1)S(1)}, bf16[1600,128]{1,0:T(8,128)(2,1)S(1)}, u32[]{:S(2)}, u32[]{:S(2)}) collective-permute-start(bf16[1600,128]{1,0:T(8,128)(2,1)S(1)} %get-tuple-element.11), channel_id=1, source_target_pairs={{0,2},{2,4},{4,6},{6,0},{128,134},{130,128},{132,130},{134,132},{2... | collective-permute-start | bytes 1228808 | tf_op jit(solution)/shard_map/ppermute | solution.py:211
  30.6 26.8 %collective-permute-start.2 = (bf16[1600,128]{1,0:T(8,128)(2,1)S(1)}, bf16[1600,128]{1,0:T(8,128)(2,1)S(1)}, u32[]{:S(2)}, u32[]{:S(2)}) collective-permute-start(bf16[1600,128]{1,0:T(8,128)(2,1)S(1)} %get-tuple-element.11), channel_id=1, source_target_pairs={{0,1},{1,0},{2,3},{3,2},{4,5},{5,4},{6,7},{7,6},{8,9},{9,8},{10,11... | collective-permute-start | bytes 1228808 | tf_op jit(solution)/shard_map/ppermute | solution.py:19
  55.4 3.6 %collective-permute-start.4 = (bf16[1600,128]{1,0:T(8,128)(2,1)S(1)}, bf16[1600,128]{1,0:T(8,128)(2,1)S(1)}, u32[]{:S(2)}, u32[]{:S(2)}) collective-permute-start(bf16[1600,128]{1,0:T(8,128)(2,1)S(1)} %collective-permute-done.3.refs_1_.refs_0_), channel_id=1, source_target_pairs={{0,1},{1,0},{2,3},{3,2},{4,5},{5,4},{6,7},{7,6},{8,9},{9,8},{10,11... | collective-permute-start | bytes 1228808 | tf_op jit(solution)/shard_map/ppermute | solution.py:19
  61.3 32.7 %all-to-all-start.1 = ((f32[8,256,128]{2,1,0:T(8,128)}), f32[8,256,128]{2,1,0:T(8,128)S(1)}, u32[]{:S(2)}, u32[]{:S(2)}) async-start(f32[8,256,128]{2,1,0:T(8,128)} %bitcast.11), calls=%async_computation.1 | async-start | bytes 2097152 | tf_op jit(solution)/shard_map/all_to_all | solution.py:219
  65.8 22.3 %collective-permute-start.6 = (bf16[1600,128]{1,0:T(8,128)(2,1)S(1)}, bf16[1600,128]{1,0:T(8,128)(2,1)S(1)}, u32[]{:S(2)}, u32[]{:S(2)}) collective-permute-start(bf16[1600,128]{1,0:T(8,128)(2,1)S(1)} %collective-permute-done.3.refs_1_.refs_0_), channel_id=1, source_target_pairs={{0,2},{2,4},{4,6},{6,0},{128,134},{130,128},{132,130},{134,132},{2... | collective-permute-start | bytes 1228808 | tf_op jit(solution)/shard_map/ppermute | solution.py:214
  88.1 3.6 %collective-permute-start.7 = (bf16[1600,128]{1,0:T(8,128)(2,1)S(1)}, bf16[1600,128]{1,0:T(8,128)(2,1)S(1)}, u32[]{:S(2)}, u32[]{:S(2)}) collective-permute-start(bf16[1600,128]{1,0:T(8,128)(2,1)S(1)} %collective-permute-done.6.refs_2_), channel_id=1, source_target_pairs={{0,1},{1,0},{2,3},{3,2},{4,5},{5,4},{6,7},{7,6},{8,9},{9,8},{10,11... | collective-permute-start | bytes 1228808 | tf_op jit(solution)/shard_map/ppermute | solution.py:19
  94.0 22.2 %all-to-all-start.2 = ((f32[16,128,128]{2,1,0:T(8,128)}), f32[16,128,128]{2,1,0:T(8,128)S(1)}, u32[]{:S(2)}, u32[]{:S(2)}) async-start(f32[16,128,128]{2,1,0:T(8,128)} %bitcast.12), calls=%async_computation.2 | async-start | bytes 2097152 | tf_op jit(solution)/shard_map/all_to_all | solution.py:219
  101.4 14.8 %collective-permute-start.5 = (f32[2,4,32,128]{3,2,1,0:T(8,128)S(1)}, f32[2,4,32,128]{3,2,1,0:T(8,128)S(1)}, u32[]{:S(2)}, u32[]{:S(2)}) collective-permute-start(f32[2,4,32,128]{3,2,1,0:T(8,128)S(1)} %shard_map.40), channel_id=1, source_target_pairs={{2,0},{4,2},{6,4},{0,6},{134,128},{128,130},{130,132},{132,134},{2... | collective-permute-start | bytes 393224 | tf_op jit(solution)/shard_map/ppermute | solution.py:235
  116.2 17.7 %copy-start.2 = (s32[32,32]{1,0:T(8,128)S(1)}, s32[32,32]{1,0:T(8,128)}, u32[]{:S(2)}) copy-start(s32[32,32]{1,0:T(8,128)} %pairs.1) | copy-start | bytes 12292
where the time goes:
time: 137 us; the launch traced here: 135 us
  waiting for transfers between devices  58.8 us (43%)
  starting transfers between devices  49.2 us (36%)
  blocking collectives  17.6 us (13%)
  Pallas kernels  7.84 us (6%)
  local copies, waits for them, and re-layouts  1.85 us (1%)
    ppermute x1, waiting for transfers between devices, patch_sums(): far = lax.ppermute(near, ('zl', 'zh'), ALONG_Z)  20.4 us
    ppermute x1, waiting for transfers between devices, patch_sums(): near = lax.ppermute(half, ('zl', 'zh'), ALONG_Z)  19.6 us
    all_to_all x1, blocking collectives, patch_sums(): lax.all_to_all(parts.reshape(16, 2 * cut, block), AUX, split_axis=0, conc...  17.6 us
    ppermute x1, starting transfers between devices, patch_sums(): outer = lax.ppermute(coeff, ROW, outward + [(b, a) for a, b in outward])  12.4 us
    all_to_all x2, starting transfers between devices, summed(): return lax.all_to_all(tiles, axes, split_axis=0, concat_axis=0, tiled=True)  11.9 us
    ppermute x4, starting transfers between devices, shifted(): lax.ppermute(value, axis, [(i, (i + step) % count) for i in range(count)])  11.1 us
    all_to_all x2, waiting for transfers between devices, summed(): return lax.all_to_all(tiles, axes, split_axis=0, concat_axis=0, tiled=True)  9.32 us
    pallas_call x7, Pallas kernels, local(): pl.pallas_call(kernel, out_shape=shapes, in_specs=[table] * scalars + [wh...  7.84 us
  transfers between devices with their start and end apart: 11, of which 6 were waited for; matrix products, arithmetic and copies ran while one was open for 0% of the time, Pallas kernels for 2%

commit v1 on v0

--- a/solution.py
+++ b/solution.py
@@ -41,22 +41,15 @@
     whole = made[...] + jnp.dot(window, sides[...], preferred_element_type=jnp.float32)
     for q in range(2):
         half[q * nocc : (q + 1) * nocc] = whole[:, q * block : (q + 1) * block].astype(half.dtype)
-    sent = [pltpu.make_async_copy(half, copies.at[k], sems.at[k]) for k in range(4)]
-    for copy in sent:
+    carried(*((half, copies.at[k], sems.at[k]) for k in range(4)))
+
+
+def carried(*moves):
+    copies = [pltpu.make_async_copy(*move) for move in moves]
+    for copy in copies:
         copy.start()
-    for copy in sent:
+    for copy in copies:
         copy.wait()
-
-
-def kept_out(kernel):
-    def run(*refs):
-        *inputs, out, made, sem = refs
-        kernel(*inputs, made)
-        copy = pltpu.make_async_copy(made, out, sem)
-        copy.start()
-        copy.wait()
-
-    return run
 
 
 def tiles_of(columns, mine):
@@ -83,33 +76,33 @@
     pl.when(jnp.logical_not(even))(lambda: store(tile.T))
 
 
-def first_tiles(own_other, near, near_other, mine, slices):
-    cut = slices.shape[4]
+def first_tiles(own_other, near, near_other, mine, slices, patch, made, near_made, sems):
+    cut = made.shape[4]
     core = lax.axis_index("c")
     own = mine.at[lax.axis_index("x")]
-    for k, made in tiles_of((own, own_other, near, near_other), mine):
+    for k, tiles in tiles_of((own, own_other, near, near_other), mine):
         for side in range(2):
-
-            def put(kind, tile, to=(core + side) % 2, k=k):
+            at = (core + side) % 2
+
+            def put(tile, at=at, k=k):
                 for s in range(4):
-                    slices[s, to, kind, k] = tile[s * cut : (s + 1) * cut]
-
-            put(0, made[side])
-            by_parity(lambda tile, put=put: put(1, tile), made[2 + side])
-
-
-def patch_tiles(near, near_other, far, far_other, mine, patch):
-    cut = patch.shape[4]
+                    made[s, at, 1, k] = tile[s * cut : (s + 1) * cut]
+                    near_made[s, k, at] = tile[s * cut : (s + 1) * cut]
+
+            for s in range(4):
+                made[s, at, 0, k] = tiles[side][s * cut : (s + 1) * cut]
+            by_parity(put, tiles[2 + side])
+    carried((made, slices, sems.at[0]), (near_made, patch.at[:, :, 0], sems.at[1]))
+
+
+def far_tiles(far, far_other, mine, patch, whole, made, sems):
+    cut = made.shape[3]
     core = lax.axis_index("c")
-    for k, made in tiles_of((near, near_other, far, far_other), mine):
+    for k, tiles in tiles_of((far, far_other), mine):
         for side in range(2):
-
-            def put(kind, tile, of=(core + side) % 2, k=k):
-                for s in range(4):
-                    patch[s, k, kind, of] = tile[s * cut : (s + 1) * cut]
-
-            put(1, made[2 + side])
-            by_parity(lambda tile, put=put: put(0, tile), made[side])
+            for s in range(4):
+                made[s, k, (core + side) % 2] = tiles[side][s * cut : (s + 1) * cut]
+    carried((made, whole.at[:, :, 1], sems.at[0]))
 
 
 def near_summed(early, out):
@@ -140,10 +133,12 @@
     row = 8 * lax.axis_index("x") + 2 * lax.axis_index("zh") + lax.axis_index("c")
     first = 8 * lax.axis_index("zl") + 2 * lax.axis_index("y")
     straight = lax.rem(lax.axis_index("y") + 4 - lax.axis_index("zh"), 4) < 2
+    kept = pairs[pl.ds(row, 1), :].astype(jnp.float32)
+    places = lax.broadcasted_iota(jnp.int32, kept.shape, 1)
     for c in range(2):
-        keep = pairs[row, first + c].astype(jnp.float32)
-        tile = (total[0, :, c] + total[1, :, c] + total[2, :, c] + total[3, :, c]) * keep
-        tile = tile.reshape(block, block)
+        keep = jnp.sum(jnp.where(places == first + c, kept, 0.0), axis=1, keepdims=True)
+        tile = total[0, :, c] + total[1, :, c] + total[2, :, c] + total[3, :, c]
+        tile = tile.reshape(block, block) * keep
 
         @pl.when(straight)
         def _(tile=tile, c=c):
@@ -154,27 +149,26 @@
             out[:, c * block : (c + 1) * block] = tile.T
 
 
-def local(kernel, results, flops, *arrays, scalars=0, out=False):
-    whole = pl.BlockSpec(memory_space=pltpu.VMEM)
-    table = pl.BlockSpec(memory_space=pltpu.SMEM)
+def local(kernel, results, flops, *arrays, scratch=(), filled=False):
+    specs = [pl.BlockSpec(memory_space=pltpu.VMEM)] * len(arrays)
+    if filled:
+        specs[-1] = pl.BlockSpec(memory_space=pltpu.HBM)
     shapes = [
         pltpu.HBM(shape, kind) if space == pltpu.HBM else jax.ShapeDtypeStruct(shape, kind)
         for shape, kind, space in results
     ]
-    scratch = []
-    if out:
-        kernel = kept_out(kernel)
-        scratch = [pltpu.VMEM(*results[0][:2]), pltpu.SemaphoreType.DMA(())]
-    elif any(space == pltpu.HBM for *_, space in results):
-        scratch = [pltpu.SemaphoreType.DMA((4,))]
+    buffers = [pltpu.VMEM(shape, jnp.float32) for shape in scratch]
+    if any(space == pltpu.HBM for *_, space in results):
+        buffers.append(pltpu.SemaphoreType.DMA((4,)))
     moved = sum(a.size * a.dtype.itemsize for a in arrays)
     moved += sum(math.prod(shape) * jnp.dtype(kind).itemsize for shape, kind, _ in results)
     return pl.pallas_call(
         kernel,
         out_shape=shapes,
-        in_specs=[table] * scalars + [whole] * (len(arrays) - scalars),
+        in_specs=specs,
         out_specs=[pl.BlockSpec(memory_space=space) for *_, space in results],
-        scratch_shapes=scratch,
+        scratch_shapes=buffers,
+        input_output_aliases={len(arrays) - 1: 0} if filled else {},
         cost_estimate=pl.CostEstimate(flops=flops, bytes_accessed=moved, transcendentals=0),
         compiler_params=pltpu.CompilerParams(vmem_limit_bytes=2 * moved + (8 << 20)),
     )(*arrays)
@@ -218,31 +212,32 @@
     def summed(tiles, axes):
         return lax.all_to_all(tiles, axes, split_axis=0, concat_axis=0, tiled=True)
 
-    work = 2 * half.shape[0] * block * 16 * block
-    (slices,) = local(
+    work = 2 * depth * block * 8 * block
+    patch_shape = (4, 4, 2, 2, cut, block)
+    slices, patch = local(
         first_tiles,
-        [((4, 2, 2, 4, cut, block), jnp.float32, hbm)],
-        work,
+        [((4, 2, 2, 4, cut, block), jnp.float32, hbm), (patch_shape, jnp.float32, hbm)],
+        2 * work,
         own_other,
         near,
         near_other,
         mine,
-        out=True,
+        scratch=[(4, 2, 2, 4, cut, block), (4, 4, 2, cut, block)],
     )
     early = summed(slices.reshape(8, 8 * cut, block), ("y", "c"))
     early = early.reshape(4, 2, 2, 4, cut, block)
     (mirrored,) = local(near_summed, [((2, 4, cut, block), jnp.float32, vmem)], 0, early)
     mirrored = lax.ppermute(mirrored, ("zl", "zh"), [(b, a) for a, b in ALONG_Z])
     (patch,) = local(
-        patch_tiles,
-        [((4, 4, 2, 2, cut, block), jnp.float32, hbm)],
+        far_tiles,
+        [(patch_shape, jnp.float32, hbm)],
         work,
-        near,
-        near_other,
         far,
         far_other,
         mine,
-        out=True,
+        patch,
+        scratch=[(4, 4, 2, cut, block)],
+        filled=True,
     )
     arrived = summed(patch.reshape(16, 4 * cut, block), ("y", "x"))
     arrived = arrived.reshape(4, 4, 2, 2, cut, block)
@@ -254,7 +249,7 @@
     )
     total = total.reshape(4, 4, 2, cut, block)
     (out,) = local(
-        finished, [((block, 2 * block), jnp.float32, vmem)], 0, pairs, total, scalars=1
+        finished, [((block, 2 * block), jnp.float32, vmem)], 0, pairs, total
     )
     return out
 

time: 137 us -> 136 us (level)
  transfers between devices with their start and end apart: 11 -> 11, of which waited for: 6 -> 6; matrix products, arithmetic and copies ran while one was open for 0% -> 0% of each run, Pallas kernels for 2% -> 1%
where the time goes in v1:
time: 136 us; the launch traced here: 134 us
  waiting for transfers between devices  58.8 us (43%)
  starting transfers between devices  49.2 us (36%)
  blocking collectives  17.6 us (13%)
  Pallas kernels  6.65 us (5%)
  local copies, waits for them, and re-layouts  1.85 us (1%)
    ppermute x1, waiting for transfers between devices, patch_sums(): far = lax.ppermute(near, ('zl', 'zh'), ALONG_Z)  20.4 us
    ppermute x1, waiting for transfers between devices, patch_sums(): near = lax.ppermute(half, ('zl', 'zh'), ALONG_Z)  19.6 us
    all_to_all x1, blocking collectives, patch_sums(): lax.all_to_all(parts.reshape(16, 2 * cut, block), AUX, split_axis=0, conc...  17.6 us
    ppermute x1, starting transfers between devices, patch_sums(): outer = lax.ppermute(coeff, ROW, outward + [(b, a) for a, b in outward])  12.4 us
    all_to_all x2, starting transfers between devices, summed(): return lax.all_to_all(tiles, axes, split_axis=0, concat_axis=0, tiled=True)  11.9 us
    ppermute x4, starting transfers between devices, shifted(): lax.ppermute(value, axis, [(i, (i + step) % count) for i in range(count)])  11.1 us
    all_to_all x2, waiting for transfers between devices, summed(): return lax.all_to_all(tiles, axes, split_axis=0, concat_axis=0, tiled=True)  9.32 us
    pallas_call x7, Pallas kernels, local(): pl.pallas_call(kernel, out_shape=shapes, in_specs=specs, out_specs=[pl.Bl...  6.65 us
  transfers between devices with their start and end apart: 11, of which 6 were waited for; matrix products, arithmetic and copies ran while one was open for 0% of the time, Pallas kernels for 1%

profile of v1, /device:TPU:6, one launch (start us, length us, event | category | flops | bytes accessed | tf_op | source)
XLA Modules:
  0.0 134.2 jit_solution(16209187426848047165)
XLA Ops:
  0.0 12.4 %collective-permute-start = (bf16[800,128]{1,0:T(8,128)(2,1)}, bf16[800,128]{1,0:T(8,128)(2,1)S(1)}, u32[]{:S(2)}, u32[]{:S(2)}) collective-permute-start(bf16[800,128]{1,0:T(8,128)(2,1)} %coeff.1), channel_id=1, source_target_pairs={{1,2},{3,4},{5,6},{7,8},{9,10},{11,12},{13,14},{15,16},{17,18},{19... | collective-permute-start | bytes 614408 | tf_op jit(solution)/shard_map/ppermute | solution.py:184
  12.4 1.9 %collective-permute-start.1 = (bf16[800,128]{1,0:T(8,128)(2,1)}, bf16[800,128]{1,0:T(8,128)(2,1)S(1)}, u32[]{:S(2)}, u32[]{:S(2)}) collective-permute-start(bf16[800,128]{1,0:T(8,128)(2,1)} %coeff.1), channel_id=1, source_target_pairs={{0,1},{1,0},{2,3},{3,2},{4,5},{5,4},{6,7},{7,6},{8,9},{9,8},{10,11... | collective-permute-start | bytes 614408 | tf_op jit(solution)/shard_map/ppermute | solution.py:19
  14.4 0.0 copy-start
  14.4 0.9 copy-done
  15.3 0.9 copy-done.1
  16.2 0.3 shard_map.37
  16.5 6.1 %collective-permute-done.outer = bf16[800,128]{1,0:T(8,128)(2,1)S(1)} collective-permute-done((bf16[800,128]{1,0:T(8,128)(2,1)}, bf16[800,128]{1,0:T(8,128)(2,1)S(1)}, u32[]{:S(2)}, u32[]{:S(2)}) %collective-permute-start) | collective-permute-done | bytes 204832 | tf_op jit(solution)/shard_map/ppermute | solution.py:184
  22.6 0.0 collective-permute-done.1.partner
  22.6 1.5 %shard_map.38 = (bf16[1600,128]{1,0:T(8,128)(2,1)S(1)}, bf16[4,1600,128]{2,1,0:T(8,128)(2,1)}) custom-call(bf16[800,128]{1,0:T(8,128)(2,1)S(1)} %collective-permute-done.outer, bf16[800,128]{1,0:T(8,128)(2,1)S(1)} %collective-permute-done.1.partner, bf16[256,256]{1,0:T(8,128)(2,1)S(1)} %get-tuple-element.11.sides, f32[800,256]{1,0:T(8,128)S(1)} %get-tuple-element.12.made), custom_call_target="tpu_custom_call" | custom-call | flops 104857600 | bytes 3407872 | tf_op jit(solution)/shard_map/pallas_call | solution.py:165
  24.1 4.5 %all-to-all-start = ((bf16[4,1600,128]{2,1,0:T(8,128)(2,1)}), bf16[4,1600,128]{2,1,0:T(8,128)(2,1)S(1)}, u32[]{:S(2)}, u32[]{:S(2)}) async-start(bf16[4,1600,128]{2,1,0:T(8,128)(2,1)} %get-tuple-element.14), calls=%async_computation | async-start | bytes 3276800 | tf_op jit(solution)/shard_map/all_to_all | solution.py:206
  28.6 1.9 %collective-permute-start.3 = (bf16[1600,128]{1,0:T(8,128)(2,1)S(1)}, bf16[1600,128]{1,0:T(8,128)(2,1)S(1)}, u32[]{:S(2)}, u32[]{:S(2)}) collective-permute-start(bf16[1600,128]{1,0:T(8,128)(2,1)S(1)} %get-tuple-element.13), channel_id=1, source_target_pairs={{0,2},{2,4},{4,6},{6,0},{128,134},{130,128},{132,130},{134,132},{2... | collective-permute-start | bytes 1228808 | tf_op jit(solution)/shard_map/ppermute | solution.py:205
  30.6 5.3 %collective-permute-start.2 = (bf16[1600,128]{1,0:T(8,128)(2,1)S(1)}, bf16[1600,128]{1,0:T(8,128)(2,1)S(1)}, u32[]{:S(2)}, u32[]{:S(2)}) collective-permute-start(bf16[1600,128]{1,0:T(8,128)(2,1)S(1)} %get-tuple-element.13), channel_id=1, source_target_pairs={{0,1},{1,0},{2,3},{3,2},{4,5},{5,4},{6,7},{7,6},{8,9},{9,8},{10,11... | collective-permute-start | bytes 1228808 | tf_op jit(solution)/shard_map/ppermute | solution.py:19
  35.9 19.6 %collective-permute-done.3.near = bf16[1600,128]{1,0:T(8,128)(2,1)S(1)} collective-permute-done((bf16[1600,128]{1,0:T(8,128)(2,1)S(1)}, bf16[1600,128]{1,0:T(8,128)(2,1)S(1)}, u32[]{:S(2)}, u32[]{:S(2)}) %collective-permute-start.3) | collective-permute-done | bytes 409632 | tf_op jit(solution)/shard_map/ppermute | solution.py:205
  55.4 1.9 %collective-permute-start.4 = (bf16[1600,128]{1,0:T(8,128)(2,1)S(1)}, bf16[1600,128]{1,0:T(8,128)(2,1)S(1)}, u32[]{:S(2)}, u32[]{:S(2)}) collective-permute-start(bf16[1600,128]{1,0:T(8,128)(2,1)S(1)} %collective-permute-done.3.near), channel_id=1, source_target_pairs={{0,1},{1,0},{2,3},{3,2},{4,5},{5,4},{6,7},{7,6},{8,9},{9,8},{10,11... | collective-permute-start | bytes 1228808 | tf_op jit(solution)/shard_map/ppermute | solution.py:19
  57.4 0.0 collective-permute-done.2.own_other
  57.4 1.7 %collective-permute-done.4.near_other = bf16[1600,128]{1,0:T(8,128)(2,1)S(1)} collective-permute-done((bf16[1600,128]{1,0:T(8,128)(2,1)S(1)}, bf16[1600,128]{1,0:T(8,128)(2,1)S(1)}, u32[]{:S(2)}, u32[]{:S(2)}) %collective-permute-start.4) | collective-permute-done | bytes 409632 | tf_op jit(solution)/shard_map/ppermute | solution.py:19
  59.1 0.0 all-to-all-done.mine
  59.1 2.5 %shard_map.39 = (f32[4,2,2,4,32,128]{5,4,3,2,1,0:T(8,128)}, f32[4,4,2,2,32,128]{5,4,3,2,1,0:T(8,128)}) custom-call(bf16[1600,128]{1,0:T(8,128)(2,1)S(1)} %collective-permute-done.2.own_other, bf16[1600,128]{1,0:T(8,128)(2,1)S(1)} %collective-permute-done.3.near, bf16[1600,128]{1,0:T(8,128)(2,1)S(1)} %collective-permute-done.4.near_other, ...), custom_call_target="tpu_custom_call" | custom-call | flops 838860800 | bytes 4964352 | tf_op jit(solution)/shard_map/pallas_call | solution.py:165
  61.5 4.5 %all-to-all-start.1 = ((f32[8,256,128]{2,1,0:T(8,128)}), f32[8,256,128]{2,1,0:T(8,128)S(1)}, u32[]{:S(2)}, u32[]{:S(2)}) async-start(f32[8,256,128]{2,1,0:T(8,128)} %bitcast.12), calls=%async_computation.1 | async-start | bytes 2097152 | tf_op jit(solution)/shard_map/all_to_all | solution.py:213
  66.0 1.9 %collective-permute-start.6 = (bf16[1600,128]{1,0:T(8,128)(2,1)S(1)}, bf16[1600,128]{1,0:T(8,128)(2,1)S(1)}, u32[]{:S(2)}, u32[]{:S(2)}) collective-permute-start(bf16[1600,128]{1,0:T(8,128)(2,1)S(1)} %collective-permute-done.3.near), channel_id=1, source_target_pairs={{0,2},{2,4},{4,6},{6,0},{128,134},{130,128},{132,130},{134,132},{2... | collective-permute-start | bytes 1228808 | tf_op jit(solution)/shard_map/ppermute | solution.py:208
  67.9 20.4 %collective-permute-done.6.far = bf16[1600,128]{1,0:T(8,128)(2,1)S(1)} collective-permute-done((bf16[1600,128]{1,0:T(8,128)(2,1)S(1)}, bf16[1600,128]{1,0:T(8,128)(2,1)S(1)}, u32[]{:S(2)}, u32[]{:S(2)}) %collective-permute-start.6) | collective-permute-done | bytes 409632 | tf_op jit(solution)/shard_map/ppermute | solution.py:208
  88.3 2.0 %collective-permute-start.7 = (bf16[1600,128]{1,0:T(8,128)(2,1)S(1)}, bf16[1600,128]{1,0:T(8,128)(2,1)S(1)}, u32[]{:S(2)}, u32[]{:S(2)}) collective-permute-start(bf16[1600,128]{1,0:T(8,128)(2,1)S(1)} %collective-permute-done.6.far), channel_id=1, source_target_pairs={{0,1},{1,0},{2,3},{3,2},{4,5},{5,4},{6,7},{7,6},{8,9},{9,8},{10,11... | collective-permute-start | bytes 1228808 | tf_op jit(solution)/shard_map/ppermute | solution.py:19
  90.3 1.7 %collective-permute-done.7.far_other = bf16[1600,128]{1,0:T(8,128)(2,1)S(1)} collective-permute-done((bf16[1600,128]{1,0:T(8,128)(2,1)S(1)}, bf16[1600,128]{1,0:T(8,128)(2,1)S(1)}, u32[]{:S(2)}, u32[]{:S(2)}) %collective-permute-start.7) | collective-permute-done | bytes 409632 | tf_op jit(solution)/shard_map/ppermute | solution.py:19
  91.9 1.5 %shard_map.41 = f32[4,4,2,2,32,128]{5,4,3,2,1,0:T(8,128)} custom-call(bf16[1600,128]{1,0:T(8,128)(2,1)S(1)} %collective-permute-done.6.far, bf16[1600,128]{1,0:T(8,128)(2,1)S(1)} %collective-permute-done.7.far_other, bf16[4,1600,128]{2,1,0:T(8,128)(2,1)S(1)} %all-to-all-done.mine, ...), custom_call_target="tpu_custom_call", output_to_operand_aliasing={{}: (3, {})} | custom-call | flops 419430400 | bytes 4554752 | tf_op jit(solution)/shard_map/pallas_call | solution.py:165
  93.5 0.0 all-to-all-done.1
  93.5 7.4 %all-to-all-start.2 = ((f32[16,128,128]{2,1,0:T(8,128)}), f32[16,128,128]{2,1,0:T(8,128)S(1)}, u32[]{:S(2)}, u32[]{:S(2)}) async-start(f32[16,128,128]{2,1,0:T(8,128)} %bitcast.11), calls=%async_computation.2 | async-start | bytes 2097152 | tf_op jit(solution)/shard_map/all_to_all | solution.py:213
  100.9 5.5 %collective-permute-start.5 = (f32[2,4,32,128]{3,2,1,0:T(8,128)S(1)}, f32[2,4,32,128]{3,2,1,0:T(8,128)S(1)}, u32[]{:S(2)}, u32[]{:S(2)}) collective-permute-start(f32[2,4,32,128]{3,2,1,0:T(8,128)S(1)} %shard_map.40), channel_id=1, source_target_pairs={{2,0},{4,2},{6,4},{0,6},{134,128},{128,130},{130,132},{132,134},{2... | collective-permute-start | bytes 393224 | tf_op jit(solution)/shard_map/ppermute | solution.py:230
  106.4 9.3 %all-to-all-done.2 = f32[16,128,128]{2,1,0:T(8,128)S(1)} async-done(((f32[16,128,128]{2,1,0:T(8,128)}), f32[16,128,128]{2,1,0:T(8,128)S(1)}, u32[]{:S(2)}, u32[]{:S(2)}) %all-to-all-start.2) | async-done | bytes 1048608 | tf_op jit(solution)/shard_map/all_to_all | solution.py:213
  115.7 0.0 collective-permute-done.5.mirrored
  115.7 0.1 shard_map.42
  115.8 17.6 %all_to_all.20 = f32[16,64,128]{2,1,0:T(8,128)S(1)} all-to-all(f32[16,64,128]{2,1,0:T(8,128)S(1)} %bitcast.10), channel_id=1, replica_groups=mesh['zl'=4,'y'=4,'x'=4,'zh'=4,'c'=2] {'zl','y'}, dimensions={0} | all-to-all | bytes 1048576 | tf_op jit(solution)/shard_map/all_to_all | solution.py:247
  133.4 0.8 shard_map.43
  (4 shorter events, 0.0 us)
Async XLA Ops:
  0.0 22.6 %collective-permute-start = (bf16[800,128]{1,0:T(8,128)(2,1)}, bf16[800,128]{1,0:T(8,128)(2,1)S(1)}, u32[]{:S(2)}, u32[]{:S(2)}) collective-permute-start(bf16[800,128]{1,0:T(8,128)(2,1)} %coeff.1), channel_id=1, source_target_pairs={{1,2},{3,4},{5,6},{7,8},{9,10},{11,12},{13,14},{15,16},{17,18},{19... | collective-permute-start | bytes 614408 | tf_op jit(solution)/shard_map/ppermute | solution.py:184
  12.4 10.2 %collective-permute-start.1 = (bf16[800,128]{1,0:T(8,128)(2,1)}, bf16[800,128]{1,0:T(8,128)(2,1)S(1)}, u32[]{:S(2)}, u32[]{:S(2)}) collective-permute-start(bf16[800,128]{1,0:T(8,128)(2,1)} %coeff.1), channel_id=1, source_target_pairs={{0,1},{1,0},{2,3},{3,2},{4,5},{5,4},{6,7},{7,6},{8,9},{9,8},{10,11... | collective-permute-start | bytes 614408 | tf_op jit(solution)/shard_map/ppermute | solution.py:19
  14.4 0.9 copy-start
  15.3 0.9 copy-start.1
  24.1 34.9 %all-to-all-start = ((bf16[4,1600,128]{2,1,0:T(8,128)(2,1)}), bf16[4,1600,128]{2,1,0:T(8,128)(2,1)S(1)}, u32[]{:S(2)}, u32[]{:S(2)}) async-start(bf16[4,1600,128]{2,1,0:T(8,128)(2,1)} %get-tuple-element.14), calls=%async_computation | async-start | bytes 3276800 | tf_op jit(solution)/shard_map/all_to_all | solution.py:206
  28.6 26.8 %collective-permute-start.3 = (bf16[1600,128]{1,0:T(8,128)(2,1)S(1)}, bf16[1600,128]{1,0:T(8,128)(2,1)S(1)}, u32[]{:S(2)}, u32[]{:S(2)}) collective-permute-start(bf16[1600,128]{1,0:T(8,128)(2,1)S(1)} %get-tuple-element.13), channel_id=1, source_target_pairs={{0,2},{2,4},{4,6},{6,0},{128,134},{130,128},{132,130},{134,132},{2... | collective-permute-start | bytes 1228808 | tf_op jit(solution)/shard_map/ppermute | solution.py:205
  30.6 26.8 %collective-permute-start.2 = (bf16[1600,128]{1,0:T(8,128)(2,1)S(1)}, bf16[1600,128]{1,0:T(8,128)(2,1)S(1)}, u32[]{:S(2)}, u32[]{:S(2)}) collective-permute-start(bf16[1600,128]{1,0:T(8,128)(2,1)S(1)} %get-tuple-element.13), channel_id=1, source_target_pairs={{0,1},{1,0},{2,3},{3,2},{4,5},{5,4},{6,7},{7,6},{8,9},{9,8},{10,11... | collective-permute-start | bytes 1228808 | tf_op jit(solution)/shard_map/ppermute | solution.py:19
  55.4 3.6 %collective-permute-start.4 = (bf16[1600,128]{1,0:T(8,128)(2,1)S(1)}, bf16[1600,128]{1,0:T(8,128)(2,1)S(1)}, u32[]{:S(2)}, u32[]{:S(2)}) collective-permute-start(bf16[1600,128]{1,0:T(8,128)(2,1)S(1)} %collective-permute-done.3.near), channel_id=1, source_target_pairs={{0,1},{1,0},{2,3},{3,2},{4,5},{5,4},{6,7},{7,6},{8,9},{9,8},{10,11... | collective-permute-start | bytes 1228808 | tf_op jit(solution)/shard_map/ppermute | solution.py:19
  61.5 31.9 %all-to-all-start.1 = ((f32[8,256,128]{2,1,0:T(8,128)}), f32[8,256,128]{2,1,0:T(8,128)S(1)}, u32[]{:S(2)}, u32[]{:S(2)}) async-start(f32[8,256,128]{2,1,0:T(8,128)} %bitcast.12), calls=%async_computation.1 | async-start | bytes 2097152 | tf_op jit(solution)/shard_map/all_to_all | solution.py:213
  66.0 22.3 %collective-permute-start.6 = (bf16[1600,128]{1,0:T(8,128)(2,1)S(1)}, bf16[1600,128]{1,0:T(8,128)(2,1)S(1)}, u32[]{:S(2)}, u32[]{:S(2)}) collective-permute-start(bf16[1600,128]{1,0:T(8,128)(2,1)S(1)} %collective-permute-done.3.near), channel_id=1, source_target_pairs={{0,2},{2,4},{4,6},{6,0},{128,134},{130,128},{132,130},{134,132},{2... | collective-permute-start | bytes 1228808 | tf_op jit(solution)/shard_map/ppermute | solution.py:208
  88.3 3.6 %collective-permute-start.7 = (bf16[1600,128]{1,0:T(8,128)(2,1)S(1)}, bf16[1600,128]{1,0:T(8,128)(2,1)S(1)}, u32[]{:S(2)}, u32[]{:S(2)}) collective-permute-start(bf16[1600,128]{1,0:T(8,128)(2,1)S(1)} %collective-permute-done.6.far), channel_id=1, source_target_pairs={{0,1},{1,0},{2,3},{3,2},{4,5},{5,4},{6,7},{7,6},{8,9},{9,8},{10,11... | collective-permute-start | bytes 1228808 | tf_op jit(solution)/shard_map/ppermute | solution.py:19
  93.5 22.2 %all-to-all-start.2 = ((f32[16,128,128]{2,1,0:T(8,128)}), f32[16,128,128]{2,1,0:T(8,128)S(1)}, u32[]{:S(2)}, u32[]{:S(2)}) async-start(f32[16,128,128]{2,1,0:T(8,128)} %bitcast.11), calls=%async_computation.2 | async-start | bytes 2097152 | tf_op jit(solution)/shard_map/all_to_all | solution.py:213
  100.9 14.8 %collective-permute-start.5 = (f32[2,4,32,128]{3,2,1,0:T(8,128)S(1)}, f32[2,4,32,128]{3,2,1,0:T(8,128)S(1)}, u32[]{:S(2)}, u32[]{:S(2)}) collective-permute-start(f32[2,4,32,128]{3,2,1,0:T(8,128)S(1)} %shard_map.40), channel_id=1, source_target_pairs={{2,0},{4,2},{6,4},{0,6},{134,128},{128,130},{130,132},{132,134},{2... | collective-permute-start | bytes 393224 | tf_op jit(solution)/shard_map/ppermute | solution.py:230
  115.7 17.7 %copy-start.2 = (s32[32,32]{1,0:T(8,128)S(1)}, s32[32,32]{1,0:T(8,128)}, u32[]{:S(2)}) copy-start(s32[32,32]{1,0:T(8,128)} %pairs.1) | copy-start | bytes 12292

commit v2 on v1

--- a/solution.py
+++ b/solution.py
@@ -76,22 +76,26 @@
     pl.when(jnp.logical_not(even))(lambda: store(tile.T))
 
 
-def first_tiles(own_other, near, near_other, mine, slices, patch, made, near_made, sems):
+def first_tiles(own_other, near, mine, near_other, slices, patch, made, near_made, fetched, sems):
     cut = made.shape[4]
     core = lax.axis_index("c")
     own = mine.at[lax.axis_index("x")]
-    for k, tiles in tiles_of((own, own_other, near, near_other), mine):
+    fetch = pltpu.make_async_copy(near_other, fetched, sems.at[2])
+    fetch.start()
+    for k, tiles in tiles_of((own, own_other), mine):
         for side in range(2):
-            at = (core + side) % 2
-
-            def put(tile, at=at, k=k):
+            for s in range(4):
+                made[s, (core + side) % 2, 0, k] = tiles[side][s * cut : (s + 1) * cut]
+    fetch.wait()
+    for k, tiles in tiles_of((near, fetched), mine):
+        for side in range(2):
+
+            def put(tile, at=(core + side) % 2, k=k):
                 for s in range(4):
                     made[s, at, 1, k] = tile[s * cut : (s + 1) * cut]
                     near_made[s, k, at] = tile[s * cut : (s + 1) * cut]
 
-            for s in range(4):
-                made[s, at, 0, k] = tiles[side][s * cut : (s + 1) * cut]
-            by_parity(put, tiles[2 + side])
+            by_parity(put, tiles[side])
     carried((made, slices, sems.at[0]), (near_made, patch.at[:, :, 0], sems.at[1]))
 
 
@@ -149,15 +153,16 @@
             out[:, c * block : (c + 1) * block] = tile.T
 
 
-def local(kernel, results, flops, *arrays, scratch=(), filled=False):
+def local(kernel, results, flops, *arrays, scratch=(), apart=False, filled=False):
     specs = [pl.BlockSpec(memory_space=pltpu.VMEM)] * len(arrays)
-    if filled:
+    if apart or filled:
+        arrays = (*arrays[:-1], pltpu.with_memory_space_constraint(arrays[-1], pltpu.HBM))
         specs[-1] = pl.BlockSpec(memory_space=pltpu.HBM)
     shapes = [
         pltpu.HBM(shape, kind) if space == pltpu.HBM else jax.ShapeDtypeStruct(shape, kind)
         for shape, kind, space in results
     ]
-    buffers = [pltpu.VMEM(shape, jnp.float32) for shape in scratch]
+    buffers = [pltpu.VMEM(shape, kind) for shape, kind in scratch]
     if any(space == pltpu.HBM for *_, space in results):
         buffers.append(pltpu.SemaphoreType.DMA((4,)))
     moved = sum(a.size * a.dtype.itemsize for a in arrays)
@@ -220,9 +225,14 @@
         2 * work,
         own_other,
         near,
+        mine,
         near_other,
-        mine,
-        scratch=[(4, 2, 2, 4, cut, block), (4, 4, 2, cut, block)],
+        scratch=[
+            ((4, 2, 2, 4, cut, block), jnp.float32),
+            ((4, 4, 2, cut, block), jnp.float32),
+            ((depth, block), jnp.bfloat16),
+        ],
+        apart=True,
     )
     early = summed(slices.reshape(8, 8 * cut, block), ("y", "c"))
     early = early.reshape(4, 2, 2, 4, cut, block)
@@ -236,7 +246,7 @@
         far_other,
         mine,
         patch,
-        scratch=[(4, 4, 2, cut, block)],
+        scratch=[((4, 4, 2, cut, block), jnp.float32)],
         filled=True,
     )
     arrived = summed(patch.reshape(16, 4 * cut, block), ("y", "x"))

time: 136 us -> 138 us (1.015)
  no operation moved by 1% of the time
where the time goes in v2:
time: 138 us; the launch traced here: 136 us
  waiting for transfers between devices  58.8 us (43%)
  starting transfers between devices  49.2 us (36%)
  blocking collectives  17.6 us (13%)
  Pallas kernels  7.28 us (5%)
  local copies, waits for them, and re-layouts  2.61 us (2%)
    ppermute x1, waiting for transfers between devices, patch_sums(): far = lax.ppermute(near, ('zl', 'zh'), ALONG_Z)  20.4 us
    ppermute x1, waiting for transfers between devices, patch_sums(): near = lax.ppermute(half, ('zl', 'zh'), ALONG_Z)  19.6 us
    all_to_all x1, blocking collectives, patch_sums(): lax.all_to_all(parts.reshape(16, 2 * cut, block), AUX, split_axis=0, conc...  17.6 us
    ppermute x1, starting transfers between devices, patch_sums(): outer = lax.ppermute(coeff, ROW, outward + [(b, a) for a, b in outward])  12.4 us
    all_to_all x2, starting transfers between devices, summed(): return lax.all_to_all(tiles, axes, split_axis=0, concat_axis=0, tiled=True)  11.9 us
    ppermute x4, starting transfers between devices, shifted(): lax.ppermute(value, axis, [(i, (i + step) % count) for i in range(count)])  11.1 us
    all_to_all x2, waiting for transfers between devices, summed(): return lax.all_to_all(tiles, axes, split_axis=0, concat_axis=0, tiled=True)  9.31 us
    pallas_call x7, Pallas kernels, local(): pl.pallas_call(kernel, out_shape=shapes, in_specs=specs, out_specs=[pl.Bl...  7.28 us
  transfers between devices with their start and end apart: 11, of which 6 were waited for; matrix products, arithmetic and copies ran while one was open for 0% of the time, Pallas kernels for 1%

profile of v2, /device:TPU:6, one launch (start us, length us, event | category | flops | bytes accessed | tf_op | source)
XLA Modules:
  0.0 135.6 jit_solution(10036828018864902816)
XLA Ops:
  0.0 12.4 %collective-permute-start = (bf16[800,128]{1,0:T(8,128)(2,1)}, bf16[800,128]{1,0:T(8,128)(2,1)S(1)}, u32[]{:S(2)}, u32[]{:S(2)}) collective-permute-start(bf16[800,128]{1,0:T(8,128)(2,1)} %coeff.1), channel_id=1, source_target_pairs={{1,2},{3,4},{5,6},{7,8},{9,10},{11,12},{13,14},{15,16},{17,18},{19... | collective-permute-start | bytes 614408 | tf_op jit(solution)/shard_map/ppermute | solution.py:189
  12.4 1.9 %collective-permute-start.1 = (bf16[800,128]{1,0:T(8,128)(2,1)}, bf16[800,128]{1,0:T(8,128)(2,1)S(1)}, u32[]{:S(2)}, u32[]{:S(2)}) collective-permute-start(bf16[800,128]{1,0:T(8,128)(2,1)} %coeff.1), channel_id=1, source_target_pairs={{0,1},{1,0},{2,3},{3,2},{4,5},{5,4},{6,7},{7,6},{8,9},{9,8},{10,11... | collective-permute-start | bytes 614408 | tf_op jit(solution)/shard_map/ppermute | solution.py:19
  14.4 0.9 copy-done
  15.3 0.9 copy-done.1
  16.2 0.3 shard_map.37
  16.5 6.1 %collective-permute-done.outer = bf16[800,128]{1,0:T(8,128)(2,1)S(1)} collective-permute-done((bf16[800,128]{1,0:T(8,128)(2,1)}, bf16[800,128]{1,0:T(8,128)(2,1)S(1)}, u32[]{:S(2)}, u32[]{:S(2)}) %collective-permute-start) | collective-permute-done | bytes 204832 | tf_op jit(solution)/shard_map/ppermute | solution.py:189
  22.6 0.0 collective-permute-done.1.partner
  22.6 1.5 %shard_map.38 = (bf16[1600,128]{1,0:T(8,128)(2,1)S(1)}, bf16[4,1600,128]{2,1,0:T(8,128)(2,1)}) custom-call(bf16[800,128]{1,0:T(8,128)(2,1)S(1)} %collective-permute-done.outer, bf16[800,128]{1,0:T(8,128)(2,1)S(1)} %collective-permute-done.1.partner, bf16[256,256]{1,0:T(8,128)(2,1)S(1)} %get-tuple-element.11.sides, f32[800,256]{1,0:T(8,128)S(1)} %get-tuple-element.12.made), custom_call_target="tpu_custom_call" | custom-call | flops 104857600 | bytes 3407872 | tf_op jit(solution)/shard_map/pallas_call | solution.py:170
  24.1 4.5 %all-to-all-start = ((bf16[4,1600,128]{2,1,0:T(8,128)(2,1)}), bf16[4,1600,128]{2,1,0:T(8,128)(2,1)S(1)}, u32[]{:S(2)}, u32[]{:S(2)}) async-start(bf16[4,1600,128]{2,1,0:T(8,128)(2,1)} %get-tuple-element.14), calls=%async_computation | async-start | bytes 3276800 | tf_op jit(solution)/shard_map/all_to_all | solution.py:211
  28.6 1.9 %collective-permute-start.3 = (bf16[1600,128]{1,0:T(8,128)(2,1)S(1)}, bf16[1600,128]{1,0:T(8,128)(2,1)S(1)}, u32[]{:S(2)}, u32[]{:S(2)}) collective-permute-start(bf16[1600,128]{1,0:T(8,128)(2,1)S(1)} %get-tuple-element.13), channel_id=1, source_target_pairs={{0,2},{2,4},{4,6},{6,0},{128,134},{130,128},{132,130},{134,132},{2... | collective-permute-start | bytes 1228808 | tf_op jit(solution)/shard_map/ppermute | solution.py:210
  30.6 5.3 %collective-permute-start.2 = (bf16[1600,128]{1,0:T(8,128)(2,1)S(1)}, bf16[1600,128]{1,0:T(8,128)(2,1)S(1)}, u32[]{:S(2)}, u32[]{:S(2)}) collective-permute-start(bf16[1600,128]{1,0:T(8,128)(2,1)S(1)} %get-tuple-element.13), channel_id=1, source_target_pairs={{0,1},{1,0},{2,3},{3,2},{4,5},{5,4},{6,7},{7,6},{8,9},{9,8},{10,11... | collective-permute-start | bytes 1228808 | tf_op jit(solution)/shard_map/ppermute | solution.py:19
  35.9 19.6 %collective-permute-done.3.near = bf16[1600,128]{1,0:T(8,128)(2,1)S(1)} collective-permute-done((bf16[1600,128]{1,0:T(8,128)(2,1)S(1)}, bf16[1600,128]{1,0:T(8,128)(2,1)S(1)}, u32[]{:S(2)}, u32[]{:S(2)}) %collective-permute-start.3) | collective-permute-done | bytes 409632 | tf_op jit(solution)/shard_map/ppermute | solution.py:210
  55.4 1.9 %collective-permute-start.4 = (bf16[1600,128]{1,0:T(8,128)(2,1)S(1)}, bf16[1600,128]{1,0:T(8,128)(2,1)S(1)}, u32[]{:S(2)}, u32[]{:S(2)}) collective-permute-start(bf16[1600,128]{1,0:T(8,128)(2,1)S(1)} %collective-permute-done.3.near), channel_id=1, source_target_pairs={{0,1},{1,0},{2,3},{3,2},{4,5},{5,4},{6,7},{7,6},{8,9},{9,8},{10,11... | collective-permute-start | bytes 1228808 | tf_op jit(solution)/shard_map/ppermute | solution.py:19
  57.3 0.0 collective-permute-done.2.own_other
  57.4 1.7 %collective-permute-done.4.near_other = bf16[1600,128]{1,0:T(8,128)(2,1)S(1)} collective-permute-done((bf16[1600,128]{1,0:T(8,128)(2,1)S(1)}, bf16[1600,128]{1,0:T(8,128)(2,1)S(1)}, u32[]{:S(2)}, u32[]{:S(2)}) %collective-permute-start.4) | collective-permute-done | bytes 409632 | tf_op jit(solution)/shard_map/ppermute | solution.py:19
  59.1 0.0 all-to-all-done.mine
  59.1 0.8 copy-done.3
  59.8 3.0 %shard_map.39 = (f32[4,2,2,4,32,128]{5,4,3,2,1,0:T(8,128)}, f32[4,4,2,2,32,128]{5,4,3,2,1,0:T(8,128)}) custom-call(bf16[1600,128]{1,0:T(8,128)(2,1)S(1)} %collective-permute-done.2.own_other, bf16[1600,128]{1,0:T(8,128)(2,1)S(1)} %collective-permute-done.3.near, bf16[4,1600,128]{2,1,0:T(8,128)(2,1)S(1)} %all-to-all-done.mine, bf16[1600,128]{1,0:T(8,128)(2,1)} %copy-done.3), custom_call_target="tpu_custom_call" | custom-call | flops 838860800 | bytes 4964352 | tf_op jit(solution)/shard_map/pallas_call | solution.py:170
  62.9 4.5 %all-to-all-start.1 = ((f32[8,256,128]{2,1,0:T(8,128)}), f32[8,256,128]{2,1,0:T(8,128)S(1)}, u32[]{:S(2)}, u32[]{:S(2)}) async-start(f32[8,256,128]{2,1,0:T(8,128)} %bitcast.12), calls=%async_computation.1 | async-start | bytes 2097152 | tf_op jit(solution)/shard_map/all_to_all | solution.py:218
  67.3 1.9 %collective-permute-start.6 = (bf16[1600,128]{1,0:T(8,128)(2,1)S(1)}, bf16[1600,128]{1,0:T(8,128)(2,1)S(1)}, u32[]{:S(2)}, u32[]{:S(2)}) collective-permute-start(bf16[1600,128]{1,0:T(8,128)(2,1)S(1)} %collective-permute-done.3.near), channel_id=1, source_target_pairs={{0,2},{2,4},{4,6},{6,0},{128,134},{130,128},{132,130},{134,132},{2... | collective-permute-start | bytes 1228808 | tf_op jit(solution)/shard_map/ppermute | solution.py:213
  69.2 20.4 %collective-permute-done.6.far = bf16[1600,128]{1,0:T(8,128)(2,1)S(1)} collective-permute-done((bf16[1600,128]{1,0:T(8,128)(2,1)S(1)}, bf16[1600,128]{1,0:T(8,128)(2,1)S(1)}, u32[]{:S(2)}, u32[]{:S(2)}) %collective-permute-start.6) | collective-permute-done | bytes 409632 | tf_op jit(solution)/shard_map/ppermute | solution.py:213
  89.6 2.0 %collective-permute-start.7 = (bf16[1600,128]{1,0:T(8,128)(2,1)S(1)}, bf16[1600,128]{1,0:T(8,128)(2,1)S(1)}, u32[]{:S(2)}, u32[]{:S(2)}) collective-permute-start(bf16[1600,128]{1,0:T(8,128)(2,1)S(1)} %collective-permute-done.6.far), channel_id=1, source_target_pairs={{0,1},{1,0},{2,3},{3,2},{4,5},{5,4},{6,7},{7,6},{8,9},{9,8},{10,11... | collective-permute-start | bytes 1228808 | tf_op jit(solution)/shard_map/ppermute | solution.py:19
  91.6 1.7 %collective-permute-done.7.far_other = bf16[1600,128]{1,0:T(8,128)(2,1)S(1)} collective-permute-done((bf16[1600,128]{1,0:T(8,128)(2,1)S(1)}, bf16[1600,128]{1,0:T(8,128)(2,1)S(1)}, u32[]{:S(2)}, u32[]{:S(2)}) %collective-permute-start.7) | collective-permute-done | bytes 409632 | tf_op jit(solution)/shard_map/ppermute | solution.py:19
  93.3 1.6 %shard_map.41 = f32[4,4,2,2,32,128]{5,4,3,2,1,0:T(8,128)} custom-call(bf16[1600,128]{1,0:T(8,128)(2,1)S(1)} %collective-permute-done.6.far, bf16[1600,128]{1,0:T(8,128)(2,1)S(1)} %collective-permute-done.7.far_other, bf16[4,1600,128]{2,1,0:T(8,128)(2,1)S(1)} %all-to-all-done.mine, ...), custom_call_target="tpu_custom_call", output_to_operand_aliasing={{}: (3, {})} | custom-call | flops 419430400 | bytes 4554752 | tf_op jit(solution)/shard_map/pallas_call | solution.py:170
  94.8 0.0 all-to-all-done.1
  94.8 7.4 %all-to-all-start.2 = ((f32[16,128,128]{2,1,0:T(8,128)}), f32[16,128,128]{2,1,0:T(8,128)S(1)}, u32[]{:S(2)}, u32[]{:S(2)}) async-start(f32[16,128,128]{2,1,0:T(8,128)} %bitcast.11), calls=%async_computation.2 | async-start | bytes 2097152 | tf_op jit(solution)/shard_map/all_to_all | solution.py:218
  102.3 5.5 %collective-permute-start.5 = (f32[2,4,32,128]{3,2,1,0:T(8,128)S(1)}, f32[2,4,32,128]{3,2,1,0:T(8,128)S(1)}, u32[]{:S(2)}, u32[]{:S(2)}) collective-permute-start(f32[2,4,32,128]{3,2,1,0:T(8,128)S(1)} %shard_map.40), channel_id=1, source_target_pairs={{2,0},{4,2},{6,4},{0,6},{134,128},{128,130},{130,132},{132,134},{2... | collective-permute-start | bytes 393224 | tf_op jit(solution)/shard_map/ppermute | solution.py:240
  107.8 9.3 %all-to-all-done.2 = f32[16,128,128]{2,1,0:T(8,128)S(1)} async-done(((f32[16,128,128]{2,1,0:T(8,128)}), f32[16,128,128]{2,1,0:T(8,128)S(1)}, u32[]{:S(2)}, u32[]{:S(2)}) %all-to-all-start.2) | async-done | bytes 1048608 | tf_op jit(solution)/shard_map/all_to_all | solution.py:218
  117.1 0.0 collective-permute-done.5.mirrored
  117.1 0.1 shard_map.42
  117.2 17.6 %all_to_all.20 = f32[16,64,128]{2,1,0:T(8,128)S(1)} all-to-all(f32[16,64,128]{2,1,0:T(8,128)S(1)} %bitcast.10), channel_id=1, replica_groups=mesh['zl'=4,'y'=4,'x'=4,'zh'=4,'c'=2] {'zl','y'}, dimensions={0} | all-to-all | bytes 1048576 | tf_op jit(solution)/shard_map/all_to_all | solution.py:257
  134.8 0.8 shard_map.43
  (6 shorter events, 0.0 us)
Async XLA Ops:
  0.0 22.6 %collective-permute-start = (bf16[800,128]{1,0:T(8,128)(2,1)}, bf16[800,128]{1,0:T(8,128)(2,1)S(1)}, u32[]{:S(2)}, u32[]{:S(2)}) collective-permute-start(bf16[800,128]{1,0:T(8,128)(2,1)} %coeff.1), channel_id=1, source_target_pairs={{1,2},{3,4},{5,6},{7,8},{9,10},{11,12},{13,14},{15,16},{17,18},{19... | collective-permute-start | bytes 614408 | tf_op jit(solution)/shard_map/ppermute | solution.py:189
  12.4 10.2 %collective-permute-start.1 = (bf16[800,128]{1,0:T(8,128)(2,1)}, bf16[800,128]{1,0:T(8,128)(2,1)S(1)}, u32[]{:S(2)}, u32[]{:S(2)}) collective-permute-start(bf16[800,128]{1,0:T(8,128)(2,1)} %coeff.1), channel_id=1, source_target_pairs={{0,1},{1,0},{2,3},{3,2},{4,5},{5,4},{6,7},{7,6},{8,9},{9,8},{10,11... | collective-permute-start | bytes 614408 | tf_op jit(solution)/shard_map/ppermute | solution.py:19
  14.4 0.9 copy-start
  15.3 0.9 copy-start.1
  24.1 34.9 %all-to-all-start = ((bf16[4,1600,128]{2,1,0:T(8,128)(2,1)}), bf16[4,1600,128]{2,1,0:T(8,128)(2,1)S(1)}, u32[]{:S(2)}, u32[]{:S(2)}) async-start(bf16[4,1600,128]{2,1,0:T(8,128)(2,1)} %get-tuple-element.14), calls=%async_computation | async-start | bytes 3276800 | tf_op jit(solution)/shard_map/all_to_all | solution.py:211
  28.6 26.8 %collective-permute-start.3 = (bf16[1600,128]{1,0:T(8,128)(2,1)S(1)}, bf16[1600,128]{1,0:T(8,128)(2,1)S(1)}, u32[]{:S(2)}, u32[]{:S(2)}) collective-permute-start(bf16[1600,128]{1,0:T(8,128)(2,1)S(1)} %get-tuple-element.13), channel_id=1, source_target_pairs={{0,2},{2,4},{4,6},{6,0},{128,134},{130,128},{132,130},{134,132},{2... | collective-permute-start | bytes 1228808 | tf_op jit(solution)/shard_map/ppermute | solution.py:210
  30.6 26.8 %collective-permute-start.2 = (bf16[1600,128]{1,0:T(8,128)(2,1)S(1)}, bf16[1600,128]{1,0:T(8,128)(2,1)S(1)}, u32[]{:S(2)}, u32[]{:S(2)}) collective-permute-start(bf16[1600,128]{1,0:T(8,128)(2,1)S(1)} %get-tuple-element.13), channel_id=1, source_target_pairs={{0,1},{1,0},{2,3},{3,2},{4,5},{5,4},{6,7},{7,6},{8,9},{9,8},{10,11... | collective-permute-start | bytes 1228808 | tf_op jit(solution)/shard_map/ppermute | solution.py:19
  55.4 3.6 %collective-permute-start.4 = (bf16[1600,128]{1,0:T(8,128)(2,1)S(1)}, bf16[1600,128]{1,0:T(8,128)(2,1)S(1)}, u32[]{:S(2)}, u32[]{:S(2)}) collective-permute-start(bf16[1600,128]{1,0:T(8,128)(2,1)S(1)} %collective-permute-done.3.near), channel_id=1, source_target_pairs={{0,1},{1,0},{2,3},{3,2},{4,5},{5,4},{6,7},{7,6},{8,9},{9,8},{10,11... | collective-permute-start | bytes 1228808 | tf_op jit(solution)/shard_map/ppermute | solution.py:19
  59.1 0.8 copy-start.3
  62.9 32.0 %all-to-all-start.1 = ((f32[8,256,128]{2,1,0:T(8,128)}), f32[8,256,128]{2,1,0:T(8,128)S(1)}, u32[]{:S(2)}, u32[]{:S(2)}) async-start(f32[8,256,128]{2,1,0:T(8,128)} %bitcast.12), calls=%async_computation.1 | async-start | bytes 2097152 | tf_op jit(solution)/shard_map/all_to_all | solution.py:218
  67.3 22.3 %collective-permute-start.6 = (bf16[1600,128]{1,0:T(8,128)(2,1)S(1)}, bf16[1600,128]{1,0:T(8,128)(2,1)S(1)}, u32[]{:S(2)}, u32[]{:S(2)}) collective-permute-start(bf16[1600,128]{1,0:T(8,128)(2,1)S(1)} %collective-permute-done.3.near), channel_id=1, source_target_pairs={{0,2},{2,4},{4,6},{6,0},{128,134},{130,128},{132,130},{134,132},{2... | collective-permute-start | bytes 1228808 | tf_op jit(solution)/shard_map/ppermute | solution.py:213
  89.6 3.6 %collective-permute-start.7 = (bf16[1600,128]{1,0:T(8,128)(2,1)S(1)}, bf16[1600,128]{1,0:T(8,128)(2,1)S(1)}, u32[]{:S(2)}, u32[]{:S(2)}) collective-permute-start(bf16[1600,128]{1,0:T(8,128)(2,1)S(1)} %collective-permute-done.6.far), channel_id=1, source_target_pairs={{0,1},{1,0},{2,3},{3,2},{4,5},{5,4},{6,7},{7,6},{8,9},{9,8},{10,11... | collective-permute-start | bytes 1228808 | tf_op jit(solution)/shard_map/ppermute | solution.py:19
  94.8 22.2 %all-to-all-start.2 = ((f32[16,128,128]{2,1,0:T(8,128)}), f32[16,128,128]{2,1,0:T(8,128)S(1)}, u32[]{:S(2)}, u32[]{:S(2)}) async-start(f32[16,128,128]{2,1,0:T(8,128)} %bitcast.11), calls=%async_computation.2 | async-start | bytes 2097152 | tf_op jit(solution)/shard_map/all_to_all | solution.py:218
  102.3 14.8 %collective-permute-start.5 = (f32[2,4,32,128]{3,2,1,0:T(8,128)S(1)}, f32[2,4,32,128]{3,2,1,0:T(8,128)S(1)}, u32[]{:S(2)}, u32[]{:S(2)}) collective-permute-start(f32[2,4,32,128]{3,2,1,0:T(8,128)S(1)} %shard_map.40), channel_id=1, source_target_pairs={{2,0},{4,2},{6,4},{0,6},{134,128},{128,130},{130,132},{132,134},{2... | collective-permute-start | bytes 393224 | tf_op jit(solution)/shard_map/ppermute | solution.py:240
  117.1 17.7 %copy-start.2 = (s32[32,32]{1,0:T(8,128)S(1)}, s32[32,32]{1,0:T(8,128)}, u32[]{:S(2)}) copy-start(s32[32,32]{1,0:T(8,128)} %pairs.1) | copy-start | bytes 12292
